TPU v7x, 32 devices: a whole 2x2x4 slice. The times are simulated.
32 devices in a mesh: sx: 8 (over z, y), sy: 4 (over x, core).
Axes of the slice: x: 2, y: 2, z: 4, core: 2. Of those that a mesh axis runs over, the one named last changes fastest.
Arguments:
- tensors: bfloat16 [2, 8, 4, 1024, 256], P(None, 'sx', 'sy'), may hold values from -6 to 6
- gates: bfloat16 [5, 2, 2, 256, 256], replicated, may hold values from -0.1875 to 0.1875
- closing_rows: bfloat16 [2, 4096, 1024], P(None, ('sx', 'sy')), may hold values from -0.125 to 0.125
- closing_columns: float32 [2, 4096, 256], P(None, ('sx', 'sy')), may hold values from -0.25 to 0.25
Outputs:
- amplitudes: float32 [2, 4096], replicated
All inputs are finite; a program needn't handle non-finite values.
Results may differ from a plain program's by a relative error of at most 0.012.
Values may be sent and summed in bfloat16 or wider, within the bound.
A program may use at most 64 MiB of HBM per device.

v0:
```python
import functools

import jax
import jax.numpy as jnp
from jax import lax
from jax.experimental import pallas as pl
from jax.experimental.pallas import tpu as pltpu
from jax.sharding import PartitionSpec as P

MESH = pl.DeviceIdType.MESH
CHUNKS = 8
LAG = 5
HOLD = 2
VECTOR = 5
FIRST = 6


def kernel(
    plan,
    x_hbm,
    g_hbm,
    u_hbm,
    v_hbm,
    out_ref,
    xs,
    xr,
    gates,
    mix,
    back,
    ubuf,
    vraw,
    vbuf,
    wbuf,
    acc,
    part,
    red,
    every,
    local_sem,
    xsend,
    xrecv,
    gsend,
    grecv,
    psend,
    precv,
    bsend,
    brecv,
):
    exchanges, gathers = plan
    rows, width2 = xs.shape[1:]
    width = width2 // 2
    slots, _, amps, _ = ubuf.shape
    step_rows = rows // CHUNKS
    coords = {"sx": lax.axis_index("sx"), "sy": lax.axis_index("sy")}

    def bit_of(axis, pos):
        return (coords[axis] // (1 << pos)) % 2

    def far(*flips):
        where = dict(coords)
        for axis, pos in flips:
            where[axis] = where[axis] + (1 << pos) * (1 - 2 * bit_of(axis, pos))
        return (where["sx"], where["sy"])

    copies = [
        pltpu.make_async_copy(x_hbm.at[0], xs.at[0, :, pl.ds(0, width)], local_sem.at[0]),
        pltpu.make_async_copy(x_hbm.at[1], xs.at[0, :, pl.ds(width, width)], local_sem.at[1]),
        pltpu.make_async_copy(v_hbm, vraw, local_sem.at[2]),
        pltpu.make_async_copy(u_hbm, ubuf.at[0], local_sem.at[3]),
        pltpu.make_async_copy(g_hbm, gates, local_sem.at[4]),
    ]
    for copy in copies:
        copy.start()

    barrier = pltpu.get_barrier_semaphore()
    peers = [(axis, pos) for axis, pos, _ in exchanges + gathers]
    for peer in peers:
        pl.semaphore_signal(barrier, inc=1, device_id=far(peer), device_id_type=MESH)
    copies[2].wait()
    vbuf[0] = vraw[...].astype(jnp.bfloat16)
    copies[0].wait()
    copies[1].wait()
    pl.semaphore_wait(barrier, len(peers))

    def x_copy(stage, chunk):
        here = pl.ds(chunk * step_rows, step_rows)
        return pltpu.make_async_remote_copy(
            src_ref=xs.at[stage, here],
            dst_ref=xr.at[stage, here],
            send_sem=xsend.at[stage, chunk],
            recv_sem=xrecv.at[stage, chunk],
            device_id=far(exchanges[stage][:2]),
            device_id_type=MESH,
        )

    def g_copy(step, slot, piece):
        landing = slot + (1 << step)
        if piece == 0:
            src, dst = vbuf.at[slot], vbuf.at[landing]
        else:
            src, dst = ubuf.at[slot, piece - 1], ubuf.at[landing, piece - 1]
        return pltpu.make_async_remote_copy(
            src_ref=src,
            dst_ref=dst,
            send_sem=gsend.at[landing, piece],
            recv_sem=grecv.at[landing, piece],
            device_id=far(gathers[step][:2]),
            device_id_type=MESH,
        )

    def offer(step):
        for piece in range(1, 3):
            g_copy(step, 0, piece).start()

    for chunk in range(CHUNKS):
        x_copy(0, chunk).start()
    for step in range(len(gathers)):
        g_copy(step, 0, 0).start()
    copies[3].wait()
    early = bit_of(*gathers[0][:2]) == bit_of(*exchanges[-1][:2])
    offer(0)
    for step in range(1, len(gathers)):
        offer(step)

    def arrive(slot, piece):
        step = slot.bit_length() - 1
        g_copy(step, slot - (1 << step), piece).wait_recv()
        for later in range(step + 1, len(gathers)):
            g_copy(later, slot, piece).start()

    copies[4].wait()
    for stage, (axis, pos, number) in enumerate(exchanges):
        sign = (1 - 2 * bit_of(axis, pos)).astype(jnp.float32).astype(jnp.bfloat16)
        for half in range(2):
            real, imag = gates[number, half, 0], gates[number, half, 1]
            if half:
                real, imag = real * sign, imag * sign
            base = half * width2
            mix[stage, pl.ds(base, width), pl.ds(0, width)] = real
            mix[stage, pl.ds(base, width), pl.ds(width, width)] = imag
            mix[stage, pl.ds(base + width, width), pl.ds(0, width)] = -imag
            mix[stage, pl.ds(base + width, width), pl.ds(width, width)] = real
    def build_back():
        for step, (axis, pos, number) in enumerate(gathers):
            sign = (2 * bit_of(axis, pos) - 1).astype(jnp.float32).astype(jnp.bfloat16)
            for half in range(2):
                real, imag = gates[number, half, 0], gates[number, half, 1]
                if half:
                    real, imag = real * sign, imag * sign
                back[step, half, pl.ds(0, width), pl.ds(0, width)] = real
                back[step, half, pl.ds(0, width), pl.ds(width, width)] = -imag
                back[step, half, pl.ds(width, width), pl.ds(0, width)] = imag
                back[step, half, pl.ds(width, width), pl.ds(width, width)] = real

    order = sorted(range(len(gathers)), key=lambda step: -gathers[step][2])

    def pull_back():
        values = [jnp.concatenate([vbuf[slot, 0], vbuf[slot, 1]], axis=-1) for slot in range(slots)]
        for place, step in enumerate(order):
            for half in range(2):
                chosen = [slot for slot in range(slots) if (slot >> step) & 1 == half]
                product = lax.dot_general(
                    jnp.concatenate([values[slot] for slot in chosen], axis=0),
                    back[step, half],
                    (((1,), (1,)), ((), ())),
                    preferred_element_type=jnp.float32,
                )
                for index, slot in enumerate(chosen):
                    rows_of = product[index * amps : (index + 1) * amps]
                    if place == len(order) - 1:
                        wbuf[slot] = rows_of
                    else:
                        values[slot] = rows_of.astype(jnp.bfloat16)

    def section(stage, chunk):
        x_copy(stage, chunk).wait_recv()
        here = pl.ds(chunk * step_rows, step_rows)
        joined = jnp.concatenate([xs[stage, here], xr[stage, here]], axis=-1)
        xs[stage + 1, here] = jnp.dot(
            joined, mix[stage], preferred_element_type=jnp.float32
        ).astype(jnp.bfloat16)
        if stage + 1 < len(exchanges):
            x_copy(stage + 1, chunk).start()

    def spread(events, moments):
        size = len(moments)
        return {
            moment: events[len(events) * place // size : len(events) * (place + 1) // size]
            for place, moment in enumerate(moments)
        }

    total = CHUNKS + LAG * (len(exchanges) - 1)
    wait_tick = total - CHUNKS + FIRST - 1
    half = slots // 2
    vectors = [(slot, 0) for slot in range(1, slots)]
    relays = [(slot, piece) for piece in range(1, 3) for slot in range(2, half) if slot % 2 == 0]
    late = [(slot, piece) for piece in range(1, 3) for slot in range(1, half) if slot % 2]
    late.sort(key=lambda event: (event[1] + event[0].bit_count(), event[0]))
    ends = [(slot, piece) for piece in range(1, 3) for slot in range(half, slots)]
    at_tick = spread(vectors, range(VECTOR))
    for events in (spread(relays, range(1, HOLD + 1)), spread(late, range(HOLD + 1, wait_tick + 1))):
        for moment in events:
            at_tick[moment] = at_tick.get(moment, []) + events[moment]

    def gather_rows(start, stop):
        return jnp.dot(
            ubuf[:, :, :, start:stop].reshape(slots * 2 * amps, stop - start),
            xs[len(exchanges), start:stop],
            preferred_element_type=jnp.float32,
        ).reshape(slots, 2, amps, 2 * width)

    for tick in range(total):
        for stage in range(len(exchanges)):
            chunk = tick - LAG * stage
            if 0 <= chunk < CHUNKS:
                section(stage, chunk)
        if tick == HOLD:
            pass
        for event in at_tick.get(tick, ()):
            arrive(*event)
        if tick == VECTOR - 1:
            build_back()
        if tick == VECTOR:
            pull_back()
        if tick == wait_tick:
            for event in ends:
                arrive(*event)
            acc[...] = gather_rows(0, FIRST * step_rows)

    def p_copy(slot):
        flips = [gathers[step][:2] for step in range(len(gathers)) if (slot >> step) & 1]
        return pltpu.make_async_remote_copy(
            src_ref=part.at[slot],
            dst_ref=red.at[slot],
            send_sem=psend.at[slot],
            recv_sem=precv.at[slot],
            device_id=far(*flips),
            device_id_type=MESH,
        )

    def fold(values):
        lanes = 128
        total_ = values[:, :lanes]
        for start in range(lanes, width, lanes):
            total_ = total_ + values[:, start : start + lanes]
        return jnp.sum(total_.T, axis=0, keepdims=True)

    acc[...] += gather_rows(FIRST * step_rows, rows)
    for slot in reversed(range(slots)):
        by_real, by_imag = acc[slot, 0], acc[slot, 1]
        proj_real = by_real[:, :width] - by_imag[:, width:]
        proj_imag = by_real[:, width:] + by_imag[:, :width]
        w_real, w_imag = wbuf[slot, :, :width], wbuf[slot, :, width:]
        part[slot, 0:1] = fold(proj_real * w_real - proj_imag * w_imag)
        part[slot, 1:2] = fold(proj_real * w_imag + proj_imag * w_real)
        if slot:
            p_copy(slot).start()

    result = part[0]
    for slot in range(1, slots):
        p_copy(slot).wait_recv()
    for slot in range(1, slots):
        result = result + red[slot]
    count_y = lax.axis_size("sy")
    count = lax.axis_size("sx") * count_y
    rank = coords["sx"] * count_y + coords["sy"]
    every[pl.ds(rank, 1)] = result[None]

    def b_copy(offset):
        other = (rank + offset) % count
        return pltpu.make_async_remote_copy(
            src_ref=every.at[rank],
            dst_ref=every.at[rank],
            send_sem=bsend.at[offset],
            recv_sem=brecv.at[offset],
            device_id=(other // count_y, other % count_y),
            device_id_type=MESH,
        )

    @pl.loop(1, count)
    def _(offset):
        b_copy(offset).start()


    for stage in range(len(exchanges)):
        for chunk in range(CHUNKS):
            x_copy(stage, chunk).wait_send()
    for step in range(len(gathers)):
        for slot in range(1 << step):
            for piece in range(3):
                g_copy(step, slot, piece).wait_send()
    for slot in range(1, slots):
        p_copy(slot).wait_send()

    @pl.loop(1, count)
    def _(offset):
        b_copy(offset).wait()

    out_ref[0] = every[:, 0, :]
    out_ref[1] = every[:, 1, :]


def local(tensors, gates, closing_rows, closing_columns):
    current = tensors[:, 0, 0]
    rows, width = current.shape[1:]
    amps = closing_rows.shape[1]
    bits_x = lax.axis_size("sx").bit_length() - 1
    bits_y = lax.axis_size("sy").bit_length() - 1
    exchanges = [("sx", pos, pos) for pos in range(bits_x - 1)]
    gathers = [("sx", bits_x - 1, bits_x - 1)]
    gathers += [("sy", pos, bits_x + pos) for pos in reversed(range(bits_y))]
    stages, steps = len(exchanges), len(gathers)
    slots = 1 << steps
    count = lax.axis_size("sx") * lax.axis_size("sy")
    closed = pl.pallas_call(
        functools.partial(kernel, (exchanges, gathers)),
        out_shape=jax.ShapeDtypeStruct((2, count, amps), jnp.float32),
        in_specs=[pl.BlockSpec(memory_space=pl.ANY)] * 4,
        out_specs=pl.BlockSpec(memory_space=pltpu.VMEM),
        scratch_shapes=[
            pltpu.VMEM((stages + 1, rows, 2 * width), jnp.bfloat16),
            pltpu.VMEM((stages, rows, 2 * width), jnp.bfloat16),
            pltpu.VMEM(gates.shape, jnp.bfloat16),
            pltpu.VMEM((stages, 4 * width, 2 * width), jnp.bfloat16),
            pltpu.VMEM((steps, 2, 2 * width, 2 * width), jnp.bfloat16),
            pltpu.VMEM((slots, 2, amps, rows), jnp.bfloat16),
            pltpu.VMEM((2, amps, width), jnp.float32),
            pltpu.VMEM((slots, 2, amps, width), jnp.bfloat16),
            pltpu.VMEM((slots, amps, 2 * width), jnp.float32),
            pltpu.VMEM((slots, 2, amps, 2 * width), jnp.float32),
            pltpu.VMEM((slots, 2, amps), jnp.float32),
            pltpu.VMEM((slots, 2, amps), jnp.float32),
            pltpu.VMEM((count, 2, amps), jnp.float32),
            pltpu.SemaphoreType.DMA((5,)),
            pltpu.SemaphoreType.DMA((stages, CHUNKS)),
            pltpu.SemaphoreType.DMA((stages, CHUNKS)),
            pltpu.SemaphoreType.DMA((slots, 3)),
            pltpu.SemaphoreType.DMA((slots, 3)),
            pltpu.SemaphoreType.DMA((slots,)),
            pltpu.SemaphoreType.DMA((slots,)),
            pltpu.SemaphoreType.DMA((count,)),
            pltpu.SemaphoreType.DMA((count,)),
        ],
        compiler_params=pltpu.CompilerParams(
            collective_id=0, has_side_effects=True, vmem_limit_bytes=60 * 2**20
        ),
    )(current, gates, closing_rows, closing_columns)
    return closed.reshape(2, count * amps)


def solution(mesh):
    placed = (
        P(None, "sx", "sy", None, None),
        P(),
        P(None, ("sx", "sy"), None),
        P(None, ("sx", "sy"), None),
    )
    return jax.shard_map(local, mesh=mesh, in_specs=placed, out_specs=P(), check_vma=False)
```

profile of v0, /device:TPU:0, one launch (start us, length us, event | category | flops | bytes accessed | tf_op | source)
XLA Modules:
  0.0 61.7 jit_solution(17593674671958650606)
XLA Ops:
  0.0 60.3 %shard_map.46 = f32[2,32,128]{2,1,0:T(8,128)} custom-call(bf16[2,1024,256]{2,1,0:T(8,128)(2,1)} %bitcast.5, bf16[5,2,2,256,256]{4,3,2,1,0:T(8,128)(2,1)} %g_hbm.1, bf16[2,128,1024]{2,1,0:T(8,128)(2,1)} %u_hbm.1, f32[2,128,256]{2,1,0:T(8,128)} %v_hbm.1), custom_call_target="tpu_custom_call" | custom-call | tf_op jit(solution)/shard_map/pallas_call | solution.py:314
  60.3 1.4 %copy.7 = f32[1,2,32,128]{3,1,2,0:T(2,128)} copy(f32[1,2,32,128]{3,2,1,0:T(8,128)} %bitcast.6) | data formatting | bytes 65536
where the time goes:
time: 61.9 us; the launch traced here: 61.7 us
  Pallas kernels  60.3 us (97%)
  local copies, waits for them, and re-layouts  1.4 us (2%)
    pallas_call x1, Pallas kernels, local(): pl.pallas_call(functools.partial(kernel, (exchanges, gathers)), out_shape...  60.3 us
    unnamed x1, local copies, waits for them, and re-layouts  1.4 us

commit v1 on v0

v1 whole, which is shorter than its diff:
```python
import functools

import jax
import jax.numpy as jnp
from jax import lax
from jax.experimental import pallas as pl
from jax.experimental.pallas import tpu as pltpu
from jax.sharding import PartitionSpec as P

MESH = pl.DeviceIdType.MESH
V, O, I = 0, 1, 2
INNER, OUTER = 0, 1
Y, Z, R, G, S, U, C, F = range(8)
FIRST = (
    (U, O), (U, I), (Y, 0), (Y, 1), (Y, 2), (Y, 3), (Y, 4), (R, 0), (R, 1), (F, V), (F, O),
    (R, 3), (R, 4), (R, 2),
)
ORDERS = (
    (
        (S, 0, 0, V), (U, 0, 0), (G, 1, 0, O), (G, 0, 3, V), (Y, 0, 0), (S, 0, 3, V),
        (G, 0, 1, V), (F,), (Y, 0, 1), (S, 0, 1, V), (U, 0, 1), (G, 0, 1, O), (G, 1, 0, I),
        (G, 1, 3, O), (G, 0, 3, O), (Y, 0, 2), (S, 1, 0, I), (R, 0), (Y, 0, 3), (G, 0, 2, V),
        (G, 0, 1, I), (R, 1), (Y, 0, 4), (G, 1, 1, O), (S, 0, 2, V), (U, 0, 2), (G, 0, 3, I),
        (G, 1, 0, V), (Y, 1, 0), (S, 0, 0, I), (S, 0, 1, I), (U, 0, 3), (G, 0, 2, O), (R, 3),
        (Y, 1, 1), (Z, 0, 1), (R, 4), (S, 0, 3, I), (S, 1, 0, V), (U, 1, 0), (Z, 0, 2),
        (G, 1, 3, I), (Y, 1, 3), (R, 2), (Z, 0, 0), (C, 0, 0, 0), (C, 1, 0, 0), (Y, 1, 4),
        (C, 0, 1, 0), (C, 0, 3, 0), (G, 0, 2, I), (G, 1, 3, V), (G, 1, 1, I), (S, 0, 2, I),
        (C, 0, 2, 0), (Y, 1, 2), (S, 1, 3, V), (U, 1, 3), (G, 1, 1, V), (S, 1, 1, I),
        (Z, 1, 0), (G, 1, 2, O), (S, 1, 3, I), (C, 1, 3, 0), (S, 1, 1, V), (U, 1, 1),
        (C, 1, 1, 0), (G, 1, 2, V), (Z, 1, 1), (C, 0, 0, 1), (C, 0, 1, 1), (C, 1, 1, 1),
        (C, 1, 3, 1), (C, 0, 2, 1), (C, 1, 0, 1), (G, 1, 2, I), (S, 1, 2, V), (U, 1, 2),
        (Z, 1, 2), (C, 0, 1, 2), (C, 0, 2, 2), (C, 0, 3, 2), (C, 1, 1, 2), (C, 1, 3, 2),
        (C, 1, 0, 2), (S, 1, 2, I), (C, 1, 2, 1), (C, 1, 2, 2), (C, 1, 2, 0), (C, 0, 0, 2),
        (C, 0, 3, 1),
    ),
    (
        (F,), (S, 0, 0, O), (S, 0, 0, V), (U, 0, 0), (G, 0, 1, V), (G, 1, 0, O), (Y, 0, 0),
        (S, 1, 0, O), (G, 0, 1, O), (S, 0, 1, V), (U, 0, 1), (S, 0, 1, O), (Y, 0, 1),
        (G, 1, 1, O), (Y, 0, 2), (G, 1, 0, I), (R, 0), (G, 0, 2, V), (S, 0, 2, V), (U, 0, 2),
        (G, 1, 2, O), (R, 1), (Y, 0, 4), (S, 1, 2, O), (Y, 0, 3), (G, 0, 2, O), (G, 1, 0, V),
        (Y, 1, 0), (S, 1, 0, V), (S, 0, 2, O), (U, 1, 0), (R, 3), (Y, 1, 1), (R, 4),
        (G, 0, 3, V), (Z, 0, 3), (S, 0, 3, V), (U, 0, 3), (Y, 1, 3), (R, 2), (Z, 0, 4),
        (C, 0, 0, 0), (C, 0, 1, 0), (C, 0, 2, 0), (G, 0, 3, O), (C, 1, 0, 0), (Y, 1, 4),
        (S, 0, 3, O), (C, 0, 3, 0), (G, 1, 1, V), (S, 1, 1, V), (Y, 1, 2), (U, 1, 1),
        (G, 1, 2, V), (Z, 1, 3), (Z, 1, 4), (C, 0, 1, 1), (C, 0, 3, 1), (C, 0, 0, 1),
        (S, 1, 2, V), (U, 1, 2), (G, 1, 3, V), (C, 1, 2, 1), (C, 1, 2, 0), (G, 1, 3, O),
        (S, 1, 1, O), (C, 1, 1, 1), (C, 0, 2, 1), (C, 1, 0, 1), (C, 1, 1, 0), (S, 1, 3, V),
        (U, 1, 3), (S, 1, 3, O), (C, 1, 3, 1), (C, 1, 3, 0),
    ),
)


def outer_rows(half):
    return max(16, half * 11 // 32 // 16 * 16)


def cut(start, size, pieces):
    units = size // 16
    marks = [start + 16 * (units * k // pieces) for k in range(pieces)] + [start + size]
    return [(marks[k], marks[k + 1] - marks[k]) for k in range(pieces) if marks[k + 1] > marks[k]]


def row_chunks(half):
    low = outer_rows(half)
    return [(INNER, *span) for span in cut(low, half - low, 3)] + [
        (OUTER, *span) for span in cut(0, low, 2)
    ]


def kernel(
    plan,
    x_hbm,
    g_hbm,
    u_hbm,
    v_hbm,
    out_ref,
    xa,
    xo,
    yr,
    zr,
    x2,
    uraw,
    uo,
    ub,
    vraw,
    vb,
    gates,
    mix,
    mixz,
    back,
    wb,
    part,
    red,
    every,
    local_sem,
    send_sem,
    xrecv,
    yrecv,
    zrecv,
    grecv,
    meet_sem,
):
    exchanges, low_bit, high_bit, split_bit, gathers = plan
    half, width2 = xo.shape
    width = width2 // 2
    amps = vb.shape[2]
    slots = vb.shape[0]
    groups = slots // 8
    stages = len(exchanges)
    chunks = row_chunks(half)
    low = outer_rows(half)
    coords = {"sx": lax.axis_index("sx"), "sy": lax.axis_index("sy")}

    def bit_of(bit):
        return (coords[bit[0]] // (1 << bit[1])) % 2

    def far(*flips):
        where = dict(coords)
        for bit in flips:
            where[bit[0]] = where[bit[0]] + (1 << bit[1]) * (1 - 2 * bit_of(bit))
        return (where["sx"], where["sy"])

    is_inner = bit_of(low_bit) != bit_of(high_bit)
    mine = bit_of(split_bit)
    own_rows = pl.ds(pl.multiple_of(mine * half, half), half)
    other_rows = pl.ds(pl.multiple_of((1 - mine) * half, half), half)

    def load(src, dst, index):
        copy = pltpu.make_async_copy(src, dst, local_sem.at[index])
        copy.start()
        return copy

    v_load = load(v_hbm, vraw, 0)
    u_loads = [
        load(u_hbm.at[:, :, own_rows], uraw.at[0], 1),
        load(u_hbm.at[:, :, other_rows], uraw.at[1], 2),
    ]
    for piece in range(2):
        lanes = pl.ds(piece * width, width)
        load(x_hbm.at[piece, own_rows], xa.at[0, 0, :, lanes], 3)
        load(x_hbm.at[piece, other_rows], xo.at[:, lanes], 4)
    g_load = load(g_hbm, gates, 5)

    barrier = pltpu.get_barrier_semaphore()
    peers = [bit for bit, _ in exchanges] + [low_bit, split_bit] + [bit for bit, _ in gathers]
    for bit in peers:
        pl.semaphore_signal(barrier, inc=1, device_id=far(bit), device_id_type=MESH)

    @pl.when(is_inner)
    def _():
        pl.semaphore_signal(barrier, inc=1, device_id=far(low_bit, high_bit), device_id_type=MESH)

    v_load.wait()
    for piece in range(2):
        vb[0, pl.ds(piece * width, width)] = vraw[piece].T.astype(jnp.bfloat16)
    for index in (1, 0):
        u_loads[index].wait()
        for piece in range(2):
            lanes = pl.ds(piece * amps, amps)
            if index:
                uo[:, lanes] = uraw[1, piece].T
            else:
                ub[0, :, lanes] = uraw[0, piece].T
    pltpu.make_async_copy(xa.at[0, 0], xa.at[0, 0], local_sem.at[3]).wait()
    pltpu.make_async_copy(xo, xo, local_sem.at[4]).wait()

    @pl.when(is_inner)
    def _():
        pl.semaphore_wait(barrier, len(peers) + 1)

    @pl.when(jnp.logical_not(is_inner))
    def _():
        pl.semaphore_wait(barrier, len(peers))

    def slot_of(group, side, place):
        return group * 8 + side * 4 + place

    def area(slot, piece):
        if piece == V:
            return vb.at[slot]
        if piece == O:
            return ub.at[slot, pl.ds(0, low)]
        return ub.at[slot, pl.ds(low, half - low)]

    LOW, ACROSS, SPLIT, GATHER = 0, 1, 2, 3
    SEND_X, SEND_U, SEND_Z, SEND_V, SEND_SHARED, SEND_O, SEND_I, SEND_Y = range(8)

    def landing_sem(role, slot, piece):
        if piece == V:
            return grecv.at[slot - 1]
        if piece == (I if role == INNER else O):
            return grecv.at[slots - 1 + slot - 1]
        return grecv.at[2 * (slots - 1) + slot - 1]

    def hop_device(hop):
        if hop == LOW:
            return far(low_bit)
        if hop == ACROSS:
            return far(low_bit, high_bit)
        if hop == SPLIT:
            return far(split_bit)
        return far(gathers[hop - GATHER][0])

    def slot_copy(role, hop, source, landing, piece, src=None):
        if src is not None:
            sender = SEND_U
        elif piece == V:
            sender = SEND_V if hop < GATHER else SEND_SHARED
        else:
            sender = SEND_O if piece == O else SEND_I
        return pltpu.make_async_remote_copy(
            src_ref=area(source, piece) if src is None else src,
            dst_ref=area(landing, piece),
            send_sem=send_sem.at[sender],
            recv_sem=landing_sem(1 - role if hop == LOW else role, landing, piece),
            device_id=hop_device(hop),
            device_id_type=MESH,
        )

    def x_copy(chunk):
        here = pl.ds(*chunks[chunk][1:])
        return pltpu.make_async_remote_copy(
            src_ref=xo.at[here],
            dst_ref=xa.at[0, 1, here],
            send_sem=send_sem.at[SEND_X],
            recv_sem=xrecv.at[chunk],
            device_id=far(split_bit),
            device_id_type=MESH,
        )

    def y_copy(stage, side, chunk):
        here = pl.ds(*chunks[chunk][1:])
        return pltpu.make_async_remote_copy(
            src_ref=xa.at[stage, side, here],
            dst_ref=yr.at[stage, side, here],
            send_sem=send_sem.at[SEND_Y + stage],
            recv_sem=yrecv.at[stage, side, chunk],
            device_id=far(exchanges[stage][0]),
            device_id_type=MESH,
        )

    def z_copy(side, chunk):
        here = pl.ds(*chunks[chunk][1:])
        return pltpu.make_async_remote_copy(
            src_ref=xa.at[stages, side, here],
            dst_ref=zr.at[side, here],
            send_sem=send_sem.at[SEND_Z],
            recv_sem=zrecv.at[side, chunk],
            device_id=far(low_bit),
            device_id_type=MESH,
        )

    def scaled(value, sign):
        return value * sign.astype(jnp.float32).astype(jnp.bfloat16)

    def build_mix():
        for stage, (bit, number) in enumerate(exchanges):
            for part_ in range(2):
                real, imag = gates[number, part_, 0], gates[number, part_, 1]
                if part_:
                    sign = 1 - 2 * bit_of(bit)
                    real, imag = scaled(real, sign), scaled(imag, sign)
                base = part_ * width2
                mix[stage, pl.ds(base, width), pl.ds(0, width)] = real
                mix[stage, pl.ds(base, width), pl.ds(width, width)] = imag
                mix[stage, pl.ds(base + width, width), pl.ds(0, width)] = -imag
                mix[stage, pl.ds(base + width, width), pl.ds(width, width)] = real

    number_low, number_high, number_split = (
        stages,
        stages + 1,
        stages + 2 + len(gathers),
    )

    def build_mixz():
        sign = 1 - 2 * bit_of(low_bit)
        for part_ in range(2):
            real, imag = gates[number_low, part_, 0], gates[number_low, part_, 1]
            for column in range(2):
                line = part_ ^ column
                r, i = real, imag
                if part_:
                    flip = sign if column == 0 else -sign
                    r, i = scaled(real, flip), scaled(imag, flip)
                base, lane = line * width2, column * width2
                mixz[pl.ds(base, width), pl.ds(lane, width)] = r
                mixz[pl.ds(base, width), pl.ds(lane + width, width)] = i
                mixz[pl.ds(base + width, width), pl.ds(lane, width)] = -i
                mixz[pl.ds(base + width, width), pl.ds(lane + width, width)] = r

    def build_back():
        bits = [(split_bit, number_split, 1)] + [(bit, number, -1) for bit, number in gathers]
        bits.append((high_bit, number_high, -1))
        for step, (bit, number, way) in enumerate(bits):
            for part_ in range(2):
                real, imag = gates[number, part_, 0], gates[number, part_, 1]
                if part_:
                    sign = way * (1 - 2 * bit_of(bit))
                    real, imag = scaled(real, sign), scaled(imag, sign)
                back[step, part_, pl.ds(0, width), pl.ds(0, width)] = real
                back[step, part_, pl.ds(0, width), pl.ds(width, width)] = -imag
                back[step, part_, pl.ds(width, width), pl.ds(0, width)] = imag
                back[step, part_, pl.ds(width, width), pl.ds(width, width)] = real

    def apply(step, part_, values):
        if amps % 128 or len(values) == 1:
            return [
                jnp.dot(back[step, part_], value, preferred_element_type=jnp.float32)
                for value in values
            ]
        product = jnp.dot(
            back[step, part_],
            jnp.concatenate(values, axis=1),
            preferred_element_type=jnp.float32,
        )
        return [product[:, k * amps : (k + 1) * amps] for k in range(len(values))]

    def rounded(values):
        return [value.astype(jnp.bfloat16) for value in values]

    def both(values):
        return apply(0, 0, values), apply(0, 1, values)

    def put(slot, values):
        for s, value in enumerate(values):
            top, bottom = pl.ds(s * width2, width), pl.ds(s * width2 + width, width)
            real, imag = value[:width], value[width:]
            wb[slot, top, pl.ds(0, amps)] = real
            wb[slot, top, pl.ds(amps, amps)] = imag
            wb[slot, bottom, pl.ds(0, amps)] = -imag
            wb[slot, bottom, pl.ds(amps, amps)] = real

    def pull_one(slot, group, side, place):
        value = vb[slot]
        (same,), (swap,) = both([value])
        same = same.astype(jnp.bfloat16)
        swap = (-swap if side else swap).astype(jnp.bfloat16)
        values = [swap, same] if side else [same, swap]
        for step in reversed(range(len(gathers))):
            matrix = back[1 + step, (group >> step) & 1]
            values = rounded(
                [jnp.dot(matrix, value, preferred_element_type=jnp.float32) for value in values]
            )
        put(slot, rounded([apply(1 + len(gathers), place >> 1, [value])[0] for value in values]))

    def pull(side, place):
        if groups > 2:
            @pl.loop(0, groups)
            def _(group):
                pull_one(group * 8 + side * 4 + place, group, side, place)

            return
        values = [vb[slot_of(group, side, place)] for group in range(groups)]
        same, swap = both(values)
        same = rounded(same)
        if side:
            swap = [-value for value in swap]
        swap = rounded(swap)
        by_side = [swap, same] if side else [same, swap]
        for step in reversed(range(len(gathers))):
            fresh = [[None] * groups, [None] * groups]
            for part_ in range(2):
                keys = [(s, g) for s in range(2) for g in range(groups) if (g >> step) & 1 == part_]
                results = rounded(apply(1 + step, part_, [by_side[s][g] for s, g in keys]))
                for (s, g), value in zip(keys, results):
                    fresh[s][g] = value
            by_side = fresh
        keys = [(s, g) for s in range(2) for g in range(groups)]
        results = rounded(
            apply(1 + len(gathers), place >> 1, [by_side[s][g] for s, g in keys])
        )
        for g in range(groups):
            put(slot_of(g, side, place), [results[s * groups + g] for s in range(2)])

    def p_copy(slot):
        group, rest = divmod(slot, 8)
        flips = [bit for step, (bit, _) in enumerate(gathers) if (group >> step) & 1]
        flips += [split_bit] if rest & 4 else []
        flips += [low_bit] if rest & 1 else []
        flips += [high_bit] if rest & 2 else []
        return pltpu.make_async_remote_copy(
            src_ref=part.at[slot],
            dst_ref=red.at[slot],
            send_sem=meet_sem.at[0],
            recv_sem=meet_sem.at[1],
            device_id=far(*flips),
            device_id_type=MESH,
        )

    def body(role):
        kept = I if role == INNER else O
        counts = {}
        begun = set()

        def start_slot(hop, source, landing, piece):
            slot_copy(role, hop, source, landing, piece).start()
            key = SEND_O if piece == O else SEND_I
            if piece == V:
                key = SEND_V if hop < GATHER else SEND_SHARED
            counts[key] = counts.get(key, 0) + 1

        def share(slot, piece):
            if piece not in (V, kept):
                return
            group = slot // 8
            for step in range(group.bit_length(), len(gathers)):
                start_slot(GATHER + step, slot, slot + 8 * (1 << step), piece)

        def forward(side, place, piece):
            slot = slot_of(0, side, place)
            if piece != V or side == 0:
                if role == OUTER:
                    if place == 0:
                        start_slot(LOW, slot, slot + 1, piece)
                else:
                    if place == 0:
                        start_slot(ACROSS, slot, slot + 3, piece)
                    if place == 1:
                        start_slot(ACROSS, slot, slot + 1, piece)
                    if place != 1 and piece != I:
                        start_slot(LOW, slot, slot_of(0, side, {0: 1, 3: 2, 2: 3}[place]), piece)
            if piece == V and side == 0:
                start_slot(SPLIT, slot, slot + 4, piece)
            share(slot, piece)

        def land(slot, piece):
            slot_copy(role, ACROSS, slot, slot, piece).wait_recv()

        def got(side, place, piece):
            land(slot_of(0, side, place), piece)
            forward(side, place, piece)

        def got_shared(side, place, piece):
            for group in range(1, groups):
                slot = slot_of(group, side, place)
                land(slot, piece)
                share(slot, piece)

        def y_section(stage, side, chunk):
            y_copy(stage, side, chunk).wait_recv()
            here = pl.ds(*chunks[chunk][1:])
            joined = jnp.concatenate([xa[stage, side, here], yr[stage, side, here]], axis=-1)
            xa[stage + 1, side, here] = jnp.dot(
                joined, mix[stage], preferred_element_type=jnp.float32
            ).astype(jnp.bfloat16)
            if stage + 1 < stages:
                y_copy(stage + 1, side, chunk).start()
            elif chunks[chunk][0] != role:
                z_copy(side, chunk).start()

        def z_section(side, chunk):
            z_copy(side, chunk).wait_recv()
            here = pl.ds(*chunks[chunk][1:])
            joined = jnp.concatenate([xa[stages, side, here], zr[side, here]], axis=-1)
            for column in range(2):
                x2[column, here, pl.ds(side * width2, width2)] = jnp.dot(
                    joined,
                    mixz[:, pl.ds(column * width2, width2)],
                    preferred_element_type=jnp.float32,
                ).astype(jnp.bfloat16)

        def relay(chunk):
            x_copy(chunk).wait_recv()
            y_copy(0, 1, chunk).start()

        def weigh(slot, here, projected, fresh):
            weight = ub[slot, here].astype(jnp.float32)
            pr, pi = projected[:, :amps], projected[:, amps:]
            ur, ui = weight[:, :amps], weight[:, amps:]
            real = jnp.sum(ur * pr - ui * pi, axis=0, keepdims=True)
            imag = jnp.sum(ur * pi + ui * pr, axis=0, keepdims=True)
            if fresh:
                part[slot, 0:1] = real
                part[slot, 1:2] = imag
            else:
                part[slot, 0:1] += real
                part[slot, 1:2] += imag

        def close(items, start, size, sides):
            here = pl.ds(start, size)
            lanes = pl.ds(sides[0] * width2, len(sides) * width2)
            if groups > 2:
                for side, place, fresh in items:
                    @pl.loop(0, groups)
                    def _(group):
                        slot = group * 8 + side * 4 + place
                        projected = jnp.dot(
                            x2[place & 1, here, lanes],
                            wb[slot, lanes],
                            preferred_element_type=jnp.float32,
                        )
                        weigh(slot, here, projected, fresh)

                return
            for parity in range(2):
                members = [
                    (slot_of(group, side, place), fresh)
                    for side, place, fresh in items
                    if place & 1 == parity
                    for group in range(groups)
                ]
                for base in range(0, len(members), 4):
                    batch = members[base : base + 4]
                    projected = jnp.dot(
                        x2[parity, here, lanes],
                        jnp.concatenate([wb[slot, lanes] for slot, _ in batch], axis=1),
                        preferred_element_type=jnp.float32,
                    )
                    for k, (slot, fresh) in enumerate(batch):
                        weigh(slot, here, projected[:, 2 * amps * k : 2 * amps * (k + 1)], fresh)

        def report(side, place):
            for group in range(groups):
                slot = slot_of(group, side, place)
                if slot:
                    p_copy(slot).start()

        for kind, which in FIRST:
            if kind == U:
                span = pl.ds(0, low) if which == O else pl.ds(low, half - low)
                slot_copy(role, SPLIT, 0, 4, which, src=uo.at[span]).start()
            elif kind == Y:
                y_copy(0, 0, which).start()
            elif kind == R:
                x_copy(which).start()
            else:
                forward(0, 0, which)

        g_load.wait()
        build_mix()
        needed = [chunk for chunk in range(len(chunks)) if chunks[chunk][0] == role]
        first = chunks[needed[0]][1]
        total = sum(chunks[chunk][2] for chunk in needed)
        head = total - chunks[needed[-1]][2] if role == INNER else total
        spans = {0: (first, total, (0,)), 1: (first, head, (1,)), 2: (first + head, total - head, (1,))}
        waiting = []
        last_part = 2 if role == INNER else 1

        def flush():
            for part_ in range(3):
                items = []
                for side, place, at_part in waiting:
                    if at_part == part_:
                        items.append((side, place, (side, place) not in begun))
                        begun.add((side, place))
                if items:
                    close(items, *spans[part_])
            for side, place, part_ in waiting:
                done[side, place] = done.get((side, place), 0) + 1
                if done[side, place] == last_part + 1:
                    report(side, place)
            waiting.clear()

        done = {}
        actions = {
            Z: z_section, R: relay, G: got, S: got_shared, U: pull, F: lambda: forward(0, 0, I),
        }
        for place, (kind, *args) in enumerate(ORDERS[role]):
            if kind == C:
                waiting.append(tuple(args))
                continue
            flush()
            if kind == U and U not in begun:
                begun.add(U)
                build_back()
            if kind == Z and Z not in begun:
                begun.add(Z)
                build_mixz()
            if kind == Y:
                for stage in range(stages):
                    y_section(stage, *args)
            else:
                actions[kind](*args)
        flush()

        def drain(index, ref):
            pltpu.make_async_copy(ref, ref, send_sem.at[index]).wait()

        drain(SEND_X, xo)
        drain(SEND_U, uo)
        for stage in range(stages):
            drain(SEND_Y + stage, xa.at[stage])
        away = pl.ds(0, low) if role == INNER else pl.ds(low, half - low)
        drain(SEND_Z, zr.at[:, away])
        for index, count_ in counts.items():
            if index in (SEND_V, SEND_SHARED):
                drain(index, vb.at[pl.ds(0, count_)])
            elif index == SEND_O:
                drain(index, ub.at[pl.ds(0, count_), pl.ds(0, low)])
            else:
                drain(index, ub.at[pl.ds(0, count_), pl.ds(low, half - low)])

    @pl.when(is_inner)
    def _():
        body(INNER)

    @pl.when(jnp.logical_not(is_inner))
    def _():
        body(OUTER)

    def meet(index, ref):
        pltpu.make_async_copy(ref, ref, meet_sem.at[index]).wait()

    result = part[0]
    meet(1, red.at[pl.ds(1, slots - 1)])
    for slot in range(1, slots):
        result = result + red[slot]
    size_x, size_y = lax.axis_size("sx"), lax.axis_size("sy")
    count = size_x * size_y
    rank = coords["sx"] * size_y + coords["sy"]
    every[pl.ds(rank, 1)] = result[None]

    def flipped(axis, mask):
        where = coords[axis]
        for bit in range(mask.bit_length()):
            if (mask >> bit) & 1:
                where = where + (1 << bit) * (1 - 2 * bit_of((axis, bit)))
        return where

    def b_copy(other):
        return pltpu.make_async_remote_copy(
            src_ref=every.at[rank],
            dst_ref=every.at[rank],
            send_sem=meet_sem.at[2],
            recv_sem=meet_sem.at[3],
            device_id=other,
            device_id_type=MESH,
        )

    if count <= 32:
        across_x = [flipped("sx", mask) for mask in range(size_x)]
        across_y = [flipped("sy", mask) for mask in range(size_y)]
        for mask in reversed(range(1, count)):
            b_copy((across_x[mask // size_y], across_y[mask % size_y])).start()
    else:

        @pl.loop(1, count)
        def _(offset):
            other = (rank + offset) % count
            b_copy((other // size_y, other % size_y)).start()

    meet(0, part.at[pl.ds(1, slots - 1)])
    meet(2, every.at[pl.ds(1, count - 1)])
    meet(3, every.at[pl.ds(1, count - 1)])

    out_ref[0] = every[:, 0, :]
    out_ref[1] = every[:, 1, :]


def local(tensors, gates, closing_rows, closing_columns):
    current = tensors[:, 0, 0]
    rows, width = current.shape[1:]
    amps = closing_rows.shape[1]
    half = rows // 2
    bits_x = lax.axis_size("sx").bit_length() - 1
    bits_y = lax.axis_size("sy").bit_length() - 1
    exchanges = [(("sx", pos), pos) for pos in range(bits_x - 2)]
    gathers = [(("sy", pos), bits_x + pos) for pos in range(bits_y - 1)]
    plan = (exchanges, ("sx", bits_x - 2), ("sx", bits_x - 1), ("sy", bits_y - 1), gathers)
    stages, steps = len(exchanges), len(gathers)
    slots = 8 << steps
    count = lax.axis_size("sx") * lax.axis_size("sy")
    chunks = len(row_chunks(half))
    closed = pl.pallas_call(
        functools.partial(kernel, plan),
        out_shape=jax.ShapeDtypeStruct((2, count, amps), jnp.float32),
        in_specs=[pl.BlockSpec(memory_space=pl.ANY)] * 4,
        out_specs=pl.BlockSpec(memory_space=pltpu.VMEM),
        scratch_shapes=[
            pltpu.VMEM((stages + 1, 2, half, 2 * width), jnp.bfloat16),
            pltpu.VMEM((half, 2 * width), jnp.bfloat16),
            pltpu.VMEM((stages, 2, half, 2 * width), jnp.bfloat16),
            pltpu.VMEM((2, half, 2 * width), jnp.bfloat16),
            pltpu.VMEM((2, half, 4 * width), jnp.bfloat16),
            pltpu.VMEM((2, 2, amps, half), jnp.bfloat16),
            pltpu.VMEM((half, 2 * amps), jnp.bfloat16),
            pltpu.VMEM((slots, half, 2 * amps), jnp.bfloat16),
            pltpu.VMEM((2, amps, width), jnp.float32),
            pltpu.VMEM((slots, 2 * width, amps), jnp.bfloat16),
            pltpu.VMEM(gates.shape, jnp.bfloat16),
            pltpu.VMEM((stages, 4 * width, 2 * width), jnp.bfloat16),
            pltpu.VMEM((4 * width, 4 * width), jnp.bfloat16),
            pltpu.VMEM((2 + steps, 2, 2 * width, 2 * width), jnp.bfloat16),
            pltpu.VMEM((slots, 4 * width, 2 * amps), jnp.bfloat16),
            pltpu.VMEM((slots, 2, amps), jnp.float32),
            pltpu.VMEM((slots, 2, amps), jnp.float32),
            pltpu.VMEM((count, 2, amps), jnp.float32),
            pltpu.SemaphoreType.DMA((6,)),
            pltpu.SemaphoreType.DMA((7 + stages,)),
            pltpu.SemaphoreType.DMA((chunks,)),
            pltpu.SemaphoreType.DMA((stages, 2, chunks)),
            pltpu.SemaphoreType.DMA((2, chunks)),
            pltpu.SemaphoreType.DMA((2 * slots + 5,)),
            pltpu.SemaphoreType.DMA((4,)),
        ],
        compiler_params=pltpu.CompilerParams(
            collective_id=0, has_side_effects=True, vmem_limit_bytes=62 * 2**20
        ),
    )(current, gates, closing_rows, closing_columns)
    return closed.reshape(2, count * amps)


def solution(mesh):
    placed = (
        P(None, "sx", "sy", None, None),
        P(),
        P(None, ("sx", "sy"), None),
        P(None, ("sx", "sy"), None),
    )
    return jax.shard_map(local, mesh=mesh, in_specs=placed, out_specs=P(), check_vma=False)
```

time: 61.9 us -> 50 us (0.81)
  Pallas kernels: 60.3 us -> 48.4 us
    pallas_call x1, Pallas kernels: 60.3 us -> 48.4 us  [local(): pl.pallas_call(functools.partial(kernel, plan), out_shape=jax.ShapeDtypeS...]
where the time goes in v1:
time: 50 us; the launch traced here: 49.8 us
  Pallas kernels  48.4 us (97%)
  local copies, waits for them, and re-layouts  1.4 us (3%)
    pallas_call x1, Pallas kernels, local(): pl.pallas_call(functools.partial(kernel, plan), out_shape=jax.ShapeDtypeS...  48.4 us
    unnamed x1, local copies, waits for them, and re-layouts  1.4 us

profile of v1, /device:TPU:0, one launch (start us, length us, event | category | flops | bytes accessed | tf_op | source)
XLA Modules:
  0.0 49.8 jit_solution(4976385217529318411)
XLA Ops:
  0.0 48.4 %shard_map.46 = f32[2,32,128]{2,1,0:T(8,128)} custom-call(bf16[2,1024,256]{2,1,0:T(8,128)(2,1)} %bitcast.5, bf16[5,2,2,256,256]{4,3,2,1,0:T(8,128)(2,1)} %g_hbm.1, bf16[2,128,1024]{2,1,0:T(8,128)(2,1)} %u_hbm.1, f32[2,128,256]{2,1,0:T(8,128)} %v_hbm.1), custom_call_target="tpu_custom_call" | custom-call | tf_op jit(solution)/shard_map/pallas_call | solution.py:664
  48.4 1.4 %copy.7 = f32[1,2,32,128]{3,1,2,0:T(2,128)} copy(f32[1,2,32,128]{3,2,1,0:T(8,128)} %bitcast.6) | data formatting | bytes 65536

commit v2 on v1

--- a/solution.py
+++ b/solution.py
@@ -661,6 +661,7 @@
     slots = 8 << steps
     count = lax.axis_size("sx") * lax.axis_size("sy")
     chunks = len(row_chunks(half))
+    grant = 55100 * 2**10 if amps % 128 == 0 else 62 * 2**20
     closed = pl.pallas_call(
         functools.partial(kernel, plan),
         out_shape=jax.ShapeDtypeStruct((2, count, amps), jnp.float32),
@@ -694,7 +695,7 @@
             pltpu.SemaphoreType.DMA((4,)),
         ],
         compiler_params=pltpu.CompilerParams(
-            collective_id=0, has_side_effects=True, vmem_limit_bytes=62 * 2**20
+            collective_id=0, has_side_effects=True, vmem_limit_bytes=grant
         ),
     )(current, gates, closing_rows, closing_columns)
     return closed.reshape(2, count * amps)

time: 50 us -> 48.6 us (0.972)
  local copies, waits for them, and re-layouts: 1.4 us -> 0.64 us
  Pallas kernels: 48.4 us -> 47.8 us
    unnamed x1, local copies, waits for them, and re-layouts: 1.4 us -> 0.64 us
    pallas_call x1, Pallas kernels: 48.4 us -> 47.8 us  [local(): pl.pallas_call(functools.partial(kernel, plan), out_shape=jax.ShapeDtypeS...]
where the time goes in v2:
time: 48.6 us; the launch traced here: 48.5 us
  Pallas kernels  47.8 us (98%)
  local copies, waits for them, and re-layouts  0.64 us (1%)
    pallas_call x1, Pallas kernels, local(): pl.pallas_call(functools.partial(kernel, plan), out_shape=jax.ShapeDtypeS...  47.8 us

profile of v2, /device:TPU:0, one launch (start us, length us, event | category | flops | bytes accessed | tf_op | source)
XLA Modules:
  0.0 48.5 jit_solution(3920237750004211904)
XLA Ops:
  0.0 47.8 %shard_map.46 = f32[2,32,128]{2,1,0:T(8,128)S(1)} custom-call(bf16[2,1024,256]{2,1,0:T(8,128)(2,1)} %bitcast.6, bf16[5,2,2,256,256]{4,3,2,1,0:T(8,128)(2,1)} %g_hbm.1, bf16[2,128,1024]{2,1,0:T(8,128)(2,1)} %u_hbm.1, f32[2,128,256]{2,1,0:T(8,128)} %v_hbm.1), custom_call_target="tpu_custom_call" | custom-call | tf_op jit(solution)/shard_map/pallas_call | solution.py:665
  47.8 0.6 %copy.7 = f32[1,2,32,128]{3,1,2,0:T(2,128)} copy(f32[1,2,32,128]{3,2,1,0:T(8,128)S(1)} %bitcast.5) | data formatting | bytes 65536

commit v3 on v2

--- a/solution.py
+++ b/solution.py
@@ -643,8 +643,12 @@
     meet(2, every.at[pl.ds(1, count - 1)])
     meet(3, every.at[pl.ds(1, count - 1)])
 
-    out_ref[0] = every[:, 0, :]
-    out_ref[1] = every[:, 1, :]
+    if len(out_ref.shape) == 2:
+        for index in range(count):
+            out_ref[:, index * amps : (index + 1) * amps] = every[index]
+    else:
+        out_ref[0] = every[:, 0, :]
+        out_ref[1] = every[:, 1, :]
 
 
 def local(tensors, gates, closing_rows, closing_columns):
@@ -661,10 +665,11 @@
     slots = 8 << steps
     count = lax.axis_size("sx") * lax.axis_size("sy")
     chunks = len(row_chunks(half))
+    shape = (2, count * amps) if amps % 128 == 0 else (2, count, amps)
     grant = 55100 * 2**10 if amps % 128 == 0 else 62 * 2**20
     closed = pl.pallas_call(
         functools.partial(kernel, plan),
-        out_shape=jax.ShapeDtypeStruct((2, count, amps), jnp.float32),
+        out_shape=jax.ShapeDtypeStruct(shape, jnp.float32),
         in_specs=[pl.BlockSpec(memory_space=pl.ANY)] * 4,
         out_specs=pl.BlockSpec(memory_space=pltpu.VMEM),
         scratch_shapes=[

time: 48.6 us -> 48.6 us (level)
  no operation moved by 1% of the time
where the time goes in v3:
time: 48.6 us; the launch traced here: 48.4 us
  Pallas kernels  47.8 us (98%)
  local copies, waits for them, and re-layouts  0.62 us (1%)
    pallas_call x1, Pallas kernels, local(): pl.pallas_call(functools.partial(kernel, plan), out_shape=jax.ShapeDtypeS...  47.8 us

profile of v3, /device:TPU:0, one launch (start us, length us, event | category | flops | bytes accessed | tf_op | source)
XLA Modules:
  0.0 48.4 jit_solution(5853298271216110040)
XLA Ops:
  0.0 47.8 %shard_map.46 = f32[2,4096]{1,0:T(2,128)S(1)} custom-call(bf16[2,1024,256]{2,1,0:T(8,128)(2,1)} %bitcast.1, bf16[5,2,2,256,256]{4,3,2,1,0:T(8,128)(2,1)} %g_hbm.1, bf16[2,128,1024]{2,1,0:T(8,128)(2,1)} %u_hbm.1, f32[2,128,256]{2,1,0:T(8,128)} %v_hbm.1), custom_call_target="tpu_custom_call" | custom-call | tf_op jit(solution)/shard_map/pallas_call | solution.py:670
  47.8 0.6 %copy.6 = f32[2,4096]{1,0:T(2,128)} copy(f32[2,4096]{1,0:T(2,128)S(1)} %shard_map.46) | data formatting | bytes 65536
